TPU v7x, 32 devices: a whole 2x2x4 slice. The times are simulated.
32 devices in a mesh: ea: 8 (over z, y), sa: 4 (over x, core).
Axes of the slice: x: 2, y: 2, z: 4, core: 2. Of those that a mesh axis runs over, the one named last changes fastest.
Arguments:
- lesser: bfloat16 [2, 1024, 2, 256, 256], P(None, 'ea', None, 'sa'), may hold values from -30 to 30, as said below
- greater: bfloat16 [2, 1024, 2, 256, 256], P(None, 'ea', None, 'sa'), may hold values from -30 to 30, as said below
Outputs:
- polar: float32 [2, 1024, 2, 256, 256], P(None, 'ea', None, 'sa')
- pol_norm: float32 [1], replicated
Inputs may be any that keep to these rules, and one draw needn't show every extreme that they name: `lesser`: Real-valued entries, independent from energy to energy. `greater`: Real-valued entries, independent from energy to energy.
All inputs are finite; a program needn't handle non-finite values.
Results may differ from a plain program's by a relative error of at most 0.0049.
Values may be sent and summed in bfloat16 or wider, within the bound.
A program may use at most 320 MiB of HBM per device.

v0:
```python
import math
import jax
import jax.numpy as jnp
from jax import lax
from jax.sharding import PartitionSpec as P

NE = 1024
ORB = 256
BLOCKS = 2


def energy_tables(count):
    index = jnp.arange(count, dtype=jnp.int32)
    phase = index[:, None] * index[None, :] % count
    angle = phase.astype(jnp.float32) * (2.0 * math.pi / count)
    return (jnp.cos(angle).astype(jnp.bfloat16), jnp.sin(angle).astype(jnp.bfloat16))


def spectra(columns, cosine, sine):
    stacked = jnp.concatenate(columns, axis=1)
    return (
        jnp.dot(cosine, stacked, preferred_element_type=jnp.float32),
        jnp.dot(sine, stacked, preferred_element_type=jnp.float32),
    )


def split_spectrum(cos_part, sin_part, which, width):
    real_cols = slice(2 * which * width, (2 * which + 1) * width)
    imag_cols = slice((2 * which + 1) * width, (2 * which + 2) * width)
    spec_re = cos_part[:, real_cols] + sin_part[:, imag_cols]
    spec_im = cos_part[:, imag_cols] - sin_part[:, real_cols]
    return (spec_re, spec_im)


def polarize(less_re, less_im, great_re, great_im, cosine, sine, count):
    width = less_re.shape[1]
    prod_re = (less_re * great_re + less_im * great_im).astype(jnp.bfloat16)
    prod_im = (less_im * great_re - less_re * great_im).astype(jnp.bfloat16)
    cos_part, sin_part = spectra([prod_re, prod_im], cosine, sine)
    corr_re = cos_part[:, :width] - sin_part[:, width:]
    corr_im = cos_part[:, width:] + sin_part[:, :width]
    weight = float(count) ** (-1.5)
    return jnp.stack([weight * corr_im, -weight * corr_re])


def both_spectra(less_pairs, great_pairs, cosine, sine):
    energies = less_pairs.shape[1]
    width = less_pairs[0].size // energies
    cos_part, sin_part = spectra(
        [
            less_pairs[0].reshape(energies, width),
            less_pairs[1].reshape(energies, width),
            great_pairs[0].reshape(energies, width),
            great_pairs[1].reshape(energies, width),
        ],
        cosine,
        sine,
    )
    less_re, less_im = split_spectrum(cos_part, sin_part, 0, width)
    great_re, great_im = split_spectrum(cos_part, sin_part, 1, width)
    return (less_re, less_im, great_re, great_im)


def body(lesser, greater):
    cosine, sine = energy_tables(NE)
    less_pairs, great_pairs = (
        lax.all_to_all(lesser, "ea", split_axis=4, concat_axis=1, tiled=True),
        lax.all_to_all(greater, "ea", split_axis=4, concat_axis=1, tiled=True),
    )
    shape = less_pairs.shape
    less_re, less_im, great_re, great_im = both_spectra(less_pairs, great_pairs, cosine, sine)
    polar_local = polarize(less_re, less_im, great_re, great_im, cosine, sine, NE).reshape(shape)
    total = jnp.sum(polar_local * polar_local)
    polar = lax.all_to_all(polar_local, "ea", split_axis=1, concat_axis=4, tiled=True)
    norm_total = lax.psum(total, ("ea", "sa"))
    pol_norm = jnp.sqrt(norm_total / (NE * BLOCKS * ORB * ORB) + 1e-06).reshape(1)
    return (polar, pol_norm)


def solution(mesh):
    return jax.shard_map(
        body,
        mesh=mesh,
        in_specs=(P(None, "ea", None, "sa", None), P(None, "ea", None, "sa", None)),
        out_specs=(P(None, "ea", None, "sa", None), P()),
        check_vma=False,
    )
```

profile of v0, /device:TPU:0, one launch (start us, length us, event | category | flops | bytes accessed | tf_op | source)
XLA Modules:
  0.0 2305.2 jit_solution(13442088749279677112)
XLA Ops:
  0.6 25.8 %copy.41 = bf16[2,128,2,64,256]{1,3,2,0,4:T(8,128)(2,1)} copy(bf16[2,128,2,64,256]{4,3,2,1,0:T(8,128)(2,1)} %param.2) | data formatting | bytes 33554432 | tf_op args[0]
  26.4 7.3 all-to-all-start
  33.7 25.9 %copy.45 = bf16[2,128,2,64,256]{1,3,2,0,4:T(8,128)(2,1)} copy(bf16[2,128,2,64,256]{4,3,2,1,0:T(8,128)(2,1)} %param.3) | data formatting | bytes 33554432 | tf_op args[1]
  59.7 337.0 %all-to-all-done = bf16[2,128,2,64,256]{1,3,2,0,4:T(8,128)(2,1)} async-done(((bf16[2,128,2,64,256]{1,3,2,0,4:T(8,128)(2,1)}), bf16[2,128,2,64,256]{1,3,2,0,4:T(8,128)(2,1)}, u32[]{:S(2)}, u32[]{:S(2)}) %all-to-all-start) | async-done | bytes 16777248 | tf_op jit(solution)/shard_map/all_to_all | solution.py:67
  396.7 5.7 all-to-all-start.1
  402.5 16.3 cosine_convert_fusion.9
  418.7 15.7 sine_convert_fusion.9
  434.4 16.3 cosine_convert_fusion.8
  450.7 16.4 sine_convert_fusion.8
  467.1 12.3 copy.42
  479.4 7.0 fusion.31
  486.4 15.1 copy.43
  501.5 15.5 copy.44
  517.0 9.4 bitcast_dynamic-update-slice_fusion.3
  526.4 238.1 %all-to-all-done.1 = bf16[2,128,2,64,256]{1,3,2,0,4:T(8,128)(2,1)} async-done(((bf16[2,128,2,64,256]{1,3,2,0,4:T(8,128)(2,1)}), bf16[2,128,2,64,256]{1,3,2,0,4:T(8,128)(2,1)}, u32[]{:S(2)}, u32[]{:S(2)}) %all-to-all-start.1) | async-done | bytes 16777248 | tf_op jit(solution)/shard_map/all_to_all | solution.py:68
  764.5 12.3 copy.46
  776.8 6.9 fusion.30
  783.7 15.1 copy.47
  798.8 15.3 copy.48
  814.1 9.4 bitcast_dynamic-update-slice_fusion.2
  823.5 9.4 bitcast_dynamic-update-slice_fusion.1
  832.9 9.8 bitcast_dynamic-update-slice_fusion
  842.7 45.0 %fusion.10 = f32[1024,16384]{1,0:T(8,128)} fusion(bf16[1024,16384]{0,1:T(8,128)(2,1)} %bitcast_dynamic-update-slice_fusion, bf16[1024,1024]{1,0:T(8,128)(2,1)} %cosine_convert_fusion.9), kind=kOutput, calls=%fused_computation.30 | convolution fusion | flops 34359738368 | bytes 102760448 | tf_op jit(solution)/shard_map/dot_general | solution.py:22
  887.7 44.3 %fusion.11 = f32[1024,16384]{1,0:T(8,128)} fusion(bf16[1024,16384]{0,1:T(8,128)(2,1)} %bitcast_dynamic-update-slice_fusion, bf16[1024,1024]{1,0:T(8,128)(2,1)S(1)} %sine_convert_fusion.9), kind=kOutput, calls=%fused_computation.31 | convolution fusion | flops 34359738368 | bytes 102760448 | tf_op jit(solution)/shard_map/dot_general | solution.py:23
  931.9 49.1 %add_convert_fusion = (bf16[1024,4096]{1,0:T(8,128)(2,1)}, bf16[1024,4096]{1,0:T(8,128)(2,1)}) fusion(f32[1024,16384]{1,0:T(8,128)} %fusion.11, f32[1024,16384]{1,0:T(8,128)} %fusion.10), kind=kLoop, calls=%fused_computation.12 | loop fusion | flops 50331648 | bytes 150994944 | tf_op jit(solution)/shard_map/convert_element_type | solution.py:37
  981.0 0.0 copy-start
  981.0 26.1 %fusion.3 = f32[1024,8192]{1,0:T(8,128)} fusion(bf16[1024,4096]{1,0:T(8,128)(2,1)} %get-tuple-element.11, bf16[1024,4096]{1,0:T(8,128)(2,1)} %get-tuple-element.10, bf16[1024,1024]{1,0:T(8,128)(2,1)} %cosine_convert_fusion.8), kind=kOutput, calls=%fused_computation.14 | convolution fusion | flops 17213423616 | bytes 52428800 | tf_op jit(solution)/shard_map/dot_general | solution.py:22
  1007.1 0.0 copy-done
  1007.1 25.7 %fusion.2 = f32[1024,8192]{1,0:T(8,128)} fusion(bf16[1024,4096]{1,0:T(8,128)(2,1)} %get-tuple-element.11, bf16[1024,4096]{1,0:T(8,128)(2,1)} %get-tuple-element.10, bf16[1024,1024]{1,0:T(8,128)(2,1)S(1)} %copy-done), kind=kOutput, calls=%fused_computation.13 | convolution fusion | flops 17213423616 | bytes 52428800 | tf_op jit(solution)/shard_map/dot_general | solution.py:23
  1032.9 34.7 %fusion.1 = (f32[1024,4096]{1,0:T(8,128)}, f32[1024,4096]{1,0:T(8,128)}) fusion(f32[1024,8192]{1,0:T(8,128)} %fusion.2, f32[1024,8192]{1,0:T(8,128)} %fusion.3), kind=kLoop, calls=%fused_computation.5 | loop fusion | flops 16777216 | bytes 100663296 | tf_op jit(solution)/shard_map/mul | solution.py:43
  1067.5 17.4 copy.49
  1085.0 17.5 copy.50
  1102.5 26.3 %multiply_reduce_fusion = (f32[]{:T(128)}, f32[2,1024,2,64,32]{1,4,3,2,0:T(8,128)}) fusion(f32[1,1024,2,64,32]{1,4,3,2,0:T(8,128)} %bitcast.50, f32[1,1024,2,64,32]{1,4,3,2,0:T(8,128)} %bitcast.49), kind=kLoop, calls=%fused_computation.1 | loop fusion | flops 25165824 | bytes 67108864 | tf_op jit(solution)/shard_map/reduce_sum | solution.py:73
  1128.7 59.1 %copy.51 = f32[2,1024,2,64,32]{3,4,2,0,1:T(8,128)} copy(f32[2,1024,2,64,32]{1,4,3,2,0:T(8,128)} %get-tuple-element.15) | data formatting | bytes 67108864 | tf_op jit(solution)/shard_map/stack | solution.py:43
  1187.8 84.9 %reshape.21 = f32[8,1,1048576]{2,1,0:T(1,128)} reshape(f32[1024,2,2,32,64]{4,3,2,1,0:T(8,128)} %bitcast.38) | data formatting | bytes 67108864
  1272.8 7.1 all-to-all-start.2
  1279.8 741.6 %psum.7 = f32[]{:T(128)} all-reduce(f32[]{:T(128)} %get-tuple-element.14), channel_id=1, replica_groups=mesh['ea'=8,'sa'=4] {'ea','sa'}, use_global_device_ids=true, to_apply=%region_1.2 | all-reduce | flops 1 | bytes 8 | tf_op jit(solution)/shard_map/psum | solution.py:75
  2022.2 0.0 all-to-all-done.2
  2022.2 0.5 broadcast.30
  2022.7 98.8 %reduce = f32[8,1048576]{1,0:T(8,128)} reduce(f32[8,1,1048576]{2,1,0:T(1,128)} %all-to-all-done.2, f32[]{:T(128)} %broadcast.30), dimensions={1}, to_apply=%all_to_all.41.reduce_sub_computation | reduce | bytes 67108864 | tf_op jit(solution)/shard_map/all_to_all | solution.py:74
  2121.5 91.3 %reshape.22 = f32[1024,2,2,32,64]{4,3,2,1,0:T(8,128)} reshape(f32[8,1048576]{1,0:T(8,128)} %reduce) | data formatting | bytes 67108864
  2212.8 56.9 %copy.53 = f32[2,128,2,64,8,32]{1,5,4,3,2,0:T(8,128)} copy(f32[2,128,2,64,8,32]{3,5,2,0,1,4:T(8,128)} %bitcast.10) | data formatting | bytes 67108864 | tf_op jit(solution)/shard_map/all_to_all | solution.py:74
  2269.8 33.8 %copy.54 = f32[2,128,2,64,256]{4,3,2,1,0:T(8,128)} copy(f32[2,128,2,64,256]{1,4,3,2,0:T(8,128)} %bitcast.48) | data formatting | bytes 67108864
Async XLA Ops:
  26.4 370.3 %all-to-all-start = ((bf16[2,128,2,64,256]{1,3,2,0,4:T(8,128)(2,1)}), bf16[2,128,2,64,256]{1,3,2,0,4:T(8,128)(2,1)}, u32[]{:S(2)}, u32[]{:S(2)}) async-start(bf16[2,128,2,64,256]{1,3,2,0,4:T(8,128)(2,1)} %copy.41), calls=%async_computation | async-start | bytes 33554432 | tf_op jit(solution)/shard_map/all_to_all | solution.py:67
  396.7 367.8 %all-to-all-start.1 = ((bf16[2,128,2,64,256]{1,3,2,0,4:T(8,128)(2,1)}), bf16[2,128,2,64,256]{1,3,2,0,4:T(8,128)(2,1)}, u32[]{:S(2)}, u32[]{:S(2)}) async-start(bf16[2,128,2,64,256]{1,3,2,0,4:T(8,128)(2,1)} %copy.45), calls=%async_computation.1 | async-start | bytes 33554432 | tf_op jit(solution)/shard_map/all_to_all | solution.py:68
  981.0 26.1 %copy-start = (bf16[1024,1024]{1,0:T(8,128)(2,1)S(1)}, bf16[1024,1024]{1,0:T(8,128)(2,1)}, u32[]{:S(2)}) copy-start(bf16[1024,1024]{1,0:T(8,128)(2,1)} %sine_convert_fusion.8) | copy-start | bytes 6291460
  1272.8 749.4 %all-to-all-start.2 = ((f32[8,1,1048576]{2,1,0:T(1,128)}), f32[8,1,1048576]{2,1,0:T(1,128)}, u32[]{:S(2)}, u32[]{:S(2)}) async-start(f32[8,1,1048576]{2,1,0:T(1,128)} %reshape.21), calls=%async_computation.2 | async-start | bytes 67108864 | tf_op jit(solution)/shard_map/all_to_all | solution.py:74
where the time goes:
time: 2320 us; the launch traced here: 2310 us
  blocking collectives  742 us (32%)
  waiting for transfers between devices  575 us (25%)
  local copies, waits for them, and re-layouts  551 us (24%)
  other arithmetic  273 us (12%)
  matrix products  141 us (6%)
    psum x1, blocking collectives, body(): norm_total = lax.psum(total, ('ea', 'sa'))  742 us
    all_to_all x1, waiting for transfers between devices, body(): lax.all_to_all(lesser, 'ea', split_axis=4, concat_axis=1, tiled=True)  337 us
    unnamed x10, local copies, waits for them, and re-layouts  290 us
    all_to_all x1, waiting for transfers between devices, body(): lax.all_to_all(greater, 'ea', split_axis=4, concat_axis=1, tiled=True)  238 us
    all_to_all x1, other arithmetic, body(): lax.all_to_all(polar_local, 'ea', split_axis=1, concat_axis=4, tiled=True)  98.8 us
    dot_general x2, matrix products, spectra(): jnp.dot(cosine, stacked, preferred_element_type=jnp.float32)  71.1 us
    dot_general x2, matrix products, spectra(): jnp.dot(sine, stacked, preferred_element_type=jnp.float32)  70 us
    another operation x1, local copies, waits for them, and re-layouts, polarize(): return jnp.stack([weight * corr_im, -weight * corr_re])  59.1 us
  transfers between devices with their start and end apart: 3, of which 2 were waited for; matrix products, arithmetic and copies ran while one was open for 6% of the time, Pallas kernels for 0%

commit v1 on v0

--- a/solution.py
+++ b/solution.py
@@ -71,7 +71,10 @@
     less_re, less_im, great_re, great_im = both_spectra(less_pairs, great_pairs, cosine, sine)
     polar_local = polarize(less_re, less_im, great_re, great_im, cosine, sine, NE).reshape(shape)
     total = jnp.sum(polar_local * polar_local)
-    polar = lax.all_to_all(polar_local, "ea", split_axis=1, concat_axis=4, tiled=True)
+    polar = jnp.concatenate(
+        lax.all_to_all(jnp.stack(jnp.split(polar_local, lax.axis_size("ea"), axis=1)), "ea", 0, 0),
+        axis=4,
+    )
     norm_total = lax.psum(total, ("ea", "sa"))
     pol_norm = jnp.sqrt(norm_total / (NE * BLOCKS * ORB * ORB) + 1e-06).reshape(1)
     return (polar, pol_norm)

time: 2320 us -> 1950 us (0.84)
  local copies, waits for them, and re-layouts: 551 us -> 290 us
  other arithmetic: 273 us -> 187 us
    unnamed x10 -> x12, local copies, waits for them, and re-layouts: 290 us -> 122 us
    all_to_all x1 -> x0, other arithmetic: 98.8 us -> none  [body(): lax.all_to_all(polar_local, 'ea', split_axis=1, concat_axis=4, tiled=True)]
    another operation x1 -> x0, local copies, waits for them, and re-layouts: 59.1 us -> none  [polarize(): return jnp.stack([weight * corr_im, -weight * corr_re])]
    all_to_all x2 -> x0, local copies, waits for them, and re-layouts: 57.5 us -> none  [body(): lax.all_to_all(polar_local, 'ea', split_axis=1, concat_axis=4, tiled=True)]
    reshape x0 -> x1, local copies, waits for them, and re-layouts: none -> 23.6 us  [body(): jnp.concatenate(lax.all_to_all(jnp.stack(jnp.split(polar_local, lax.axis_...]
  transfers between devices with their start and end apart: 3 -> 3, of which waited for: 2 -> 2; matrix products, arithmetic and copies ran while one was open for 6% -> 9% of each run, Pallas kernels for 0% -> 0%
where the time goes in v1:
time: 1950 us; the launch traced here: 1940 us
  blocking collectives  726 us (37%)
  waiting for transfers between devices  575 us (29%)
  local copies, waits for them, and re-layouts  290 us (15%)
  other arithmetic  187 us (10%)
  matrix products  141 us (7%)
  starting transfers between devices  20.4 us (1%)
    psum x1, blocking collectives, body(): norm_total = lax.psum(total, ('ea', 'sa'))  726 us
    all_to_all x1, waiting for transfers between devices, body(): lax.all_to_all(lesser, 'ea', split_axis=4, concat_axis=1, tiled=True)  337 us
    all_to_all x1, waiting for transfers between devices, body(): lax.all_to_all(greater, 'ea', split_axis=4, concat_axis=1, tiled=True)  238 us
    unnamed x12, local copies, waits for them, and re-layouts  122 us
    dot_general x2, matrix products, spectra(): jnp.dot(cosine, stacked, preferred_element_type=jnp.float32)  71 us
    dot_general x2, matrix products, spectra(): jnp.dot(sine, stacked, preferred_element_type=jnp.float32)  69.9 us
    convert_element_type x1, other arithmetic, polarize(): prod_re = (less_re * great_re + less_im * great_im).astype(jnp.bfloat16)  49.3 us
  transfers between devices with their start and end apart: 3, of which 2 were waited for; matrix products, arithmetic and copies ran while one was open for 9% of the time, Pallas kernels for 0%

profile of v1, /device:TPU:0, one launch (start us, length us, event | category | flops | bytes accessed | tf_op | source)
XLA Modules:
  0.0 1942.7 jit_solution(9563622262076796038)
XLA Ops:
  0.6 25.8 %copy.15 = bf16[2,128,2,64,256]{1,3,2,0,4:T(8,128)(2,1)} copy(bf16[2,128,2,64,256]{4,3,2,1,0:T(8,128)(2,1)} %param.2) | data formatting | bytes 33554432 | tf_op args[0]
  26.4 7.3 all-to-all-start
  33.7 25.9 %copy.19 = bf16[2,128,2,64,256]{1,3,2,0,4:T(8,128)(2,1)} copy(bf16[2,128,2,64,256]{4,3,2,1,0:T(8,128)(2,1)} %param.3) | data formatting | bytes 33554432 | tf_op args[1]
  59.7 337.0 %all-to-all-done = bf16[2,128,2,64,256]{1,3,2,0,4:T(8,128)(2,1)} async-done(((bf16[2,128,2,64,256]{1,3,2,0,4:T(8,128)(2,1)}), bf16[2,128,2,64,256]{1,3,2,0,4:T(8,128)(2,1)}, u32[]{:S(2)}, u32[]{:S(2)}) %all-to-all-start) | async-done | bytes 16777248 | tf_op jit(solution)/shard_map/all_to_all | solution.py:67
  396.7 5.8 all-to-all-start.1
  402.5 16.3 cosine_convert_fusion.9
  418.7 15.7 sine_convert_fusion.9
  434.4 16.2 cosine_convert_fusion.8
  450.7 16.4 sine_convert_fusion.8
  467.0 12.3 copy.16
  479.4 7.0 fusion.57
  486.4 15.1 copy.17
  501.5 15.3 copy.18
  516.7 9.4 bitcast_dynamic-update-slice_fusion.3
  526.2 238.4 %all-to-all-done.1 = bf16[2,128,2,64,256]{1,3,2,0,4:T(8,128)(2,1)} async-done(((bf16[2,128,2,64,256]{1,3,2,0,4:T(8,128)(2,1)}), bf16[2,128,2,64,256]{1,3,2,0,4:T(8,128)(2,1)}, u32[]{:S(2)}, u32[]{:S(2)}) %all-to-all-start.1) | async-done | bytes 16777248 | tf_op jit(solution)/shard_map/all_to_all | solution.py:68
  764.5 12.3 copy.20
  776.8 7.2 fusion.56
  784.0 15.1 copy.21
  799.1 15.3 copy.22
  814.4 9.4 bitcast_dynamic-update-slice_fusion.2
  823.8 9.4 bitcast_dynamic-update-slice_fusion.1
  833.2 9.6 bitcast_dynamic-update-slice_fusion
  842.8 44.9 %fusion.36 = f32[1024,16384]{1,0:T(8,128)} fusion(bf16[1024,16384]{0,1:T(8,128)(2,1)} %bitcast_dynamic-update-slice_fusion, bf16[1024,1024]{1,0:T(8,128)(2,1)} %cosine_convert_fusion.9), kind=kOutput, calls=%fused_computation.71 | convolution fusion | flops 34359738368 | bytes 102760448 | tf_op jit(solution)/shard_map/dot_general | solution.py:22
  887.7 44.2 %fusion.37 = f32[1024,16384]{1,0:T(8,128)} fusion(bf16[1024,16384]{0,1:T(8,128)(2,1)} %bitcast_dynamic-update-slice_fusion, bf16[1024,1024]{1,0:T(8,128)(2,1)S(1)} %sine_convert_fusion.9), kind=kOutput, calls=%fused_computation.72 | convolution fusion | flops 34359738368 | bytes 102760448 | tf_op jit(solution)/shard_map/dot_general | solution.py:23
  931.9 49.3 %add_convert_fusion = (bf16[1024,4096]{1,0:T(8,128)(2,1)}, bf16[1024,4096]{1,0:T(8,128)(2,1)}) fusion(f32[1024,16384]{1,0:T(8,128)} %fusion.37, f32[1024,16384]{1,0:T(8,128)} %fusion.36), kind=kLoop, calls=%fused_computation.29 | loop fusion | flops 50331648 | bytes 150994944 | tf_op jit(solution)/shard_map/convert_element_type | solution.py:37
  981.2 0.0 copy-start.2
  981.2 26.1 %fusion.5 = f32[1024,8192]{1,0:T(8,128)} fusion(bf16[1024,4096]{1,0:T(8,128)(2,1)} %get-tuple-element.7, bf16[1024,4096]{1,0:T(8,128)(2,1)} %get-tuple-element.6, bf16[1024,1024]{1,0:T(8,128)(2,1)} %cosine_convert_fusion.8), kind=kOutput, calls=%fused_computation.31 | convolution fusion | flops 17213423616 | bytes 52428800 | tf_op jit(solution)/shard_map/dot_general | solution.py:22
  1007.3 0.0 copy-done.2
  1007.3 25.7 %fusion.4 = f32[1024,8192]{1,0:T(8,128)} fusion(bf16[1024,4096]{1,0:T(8,128)(2,1)} %get-tuple-element.7, bf16[1024,4096]{1,0:T(8,128)(2,1)} %get-tuple-element.6, bf16[1024,1024]{1,0:T(8,128)(2,1)S(1)} %copy-done.2), kind=kOutput, calls=%fused_computation.30 | convolution fusion | flops 17213423616 | bytes 52428800 | tf_op jit(solution)/shard_map/dot_general | solution.py:23
  1033.0 34.7 %fusion.2 = (f32[1024,4096]{1,0:T(8,128)}, f32[1024,4096]{1,0:T(8,128)}) fusion(f32[1024,8192]{1,0:T(8,128)} %fusion.4, f32[1024,8192]{1,0:T(8,128)} %fusion.5), kind=kLoop, calls=%fused_computation.20 | loop fusion | flops 16777216 | bytes 100663296 | tf_op jit(solution)/shard_map/mul | solution.py:43
  1067.7 17.4 copy.23
  1085.1 17.4 copy.24
  1102.6 5.0 fusion.11
  1107.6 3.6 copy-done
  1111.2 4.8 copy-done.1
  1115.9 2.6 fusion.14
  1118.5 2.6 fusion.17
  1121.2 2.6 fusion.20
  1123.8 2.6 fusion.23
  1126.4 2.6 fusion.26
  1129.0 2.6 fusion.29
  1131.6 2.6 fusion.32
  1134.3 7.3 all-to-all-start.2
  1141.6 15.6 fusion.1
  1157.2 726.0 %psum.7 = f32[]{:T(128)} all-reduce(f32[]{:T(128)} %fusion.1), channel_id=1, replica_groups=mesh['ea'=8,'sa'=4] {'ea','sa'}, use_global_device_ids=true, to_apply=%region_1.2 | all-reduce | flops 1 | bytes 8 | tf_op jit(solution)/shard_map/psum | solution.py:78
  1883.9 0.0 all-to-all-done.2
  1883.9 23.6 %copy.25 = f32[2,128,2,64,8,32]{1,5,4,3,2,0:T(8,128)} copy(f32[2,128,2,64,8,32]{1,5,3,2,0,4:T(8,128)} %bitcast.16) | data formatting | bytes 67108864 | tf_op jit(solution)/shard_map/reshape | solution.py:74
  1907.5 33.8 %copy.26 = f32[2,128,2,64,256]{4,3,2,1,0:T(8,128)} copy(f32[2,128,2,64,256]{1,4,3,2,0:T(8,128)} %bitcast.93) | data formatting | bytes 67108864
  (2 shorter events, 0.0 us)
Async XLA Ops:
  26.4 370.3 %all-to-all-start = ((bf16[2,128,2,64,256]{1,3,2,0,4:T(8,128)(2,1)}), bf16[2,128,2,64,256]{1,3,2,0,4:T(8,128)(2,1)}, u32[]{:S(2)}, u32[]{:S(2)}) async-start(bf16[2,128,2,64,256]{1,3,2,0,4:T(8,128)(2,1)} %copy.15), calls=%async_computation | async-start | bytes 33554432 | tf_op jit(solution)/shard_map/all_to_all | solution.py:67
  396.7 367.8 %all-to-all-start.1 = ((bf16[2,128,2,64,256]{1,3,2,0,4:T(8,128)(2,1)}), bf16[2,128,2,64,256]{1,3,2,0,4:T(8,128)(2,1)}, u32[]{:S(2)}, u32[]{:S(2)}) async-start(bf16[2,128,2,64,256]{1,3,2,0,4:T(8,128)(2,1)} %copy.19), calls=%async_computation.1 | async-start | bytes 33554432 | tf_op jit(solution)/shard_map/all_to_all | solution.py:68
  981.2 26.1 %copy-start.2 = (bf16[1024,1024]{1,0:T(8,128)(2,1)S(1)}, bf16[1024,1024]{1,0:T(8,128)(2,1)}, u32[]{:S(2)}) copy-start(bf16[1024,1024]{1,0:T(8,128)(2,1)} %sine_convert_fusion.8) | copy-start | bytes 6291460
  1102.6 8.6 copy-start
  1102.6 13.3 copy-start.1
  1134.3 749.7 %all-to-all-start.2 = ((f32[8,2,128,2,64,32]{2,5,4,3,1,0:T(8,128)}), f32[8,2,128,2,64,32]{2,5,4,3,1,0:T(8,128)}, u32[]{:S(2)}, u32[]{:S(2)}) async-start(f32[8,2,128,2,64,32]{2,5,4,3,1,0:T(8,128)} %fusion.32), calls=%async_computation.2 | async-start | bytes 67108864 | tf_op jit(solution)/shard_map/all_to_all | solution.py:75
